TPU v7x, 32 devices: a whole 2x2x4 slice. The times are simulated.
32 devices in a mesh: blk: 8 (over z, x), ga: 4 (over y, core).
Axes of the slice: x: 2, y: 2, z: 4, core: 2. Of those that a mesh axis runs over, the one named last changes fastest.
Arguments:
- pair_val: bfloat16 [16, 16, 16, 2048], P('blk', None, None, 'ga'), may hold values from -0.125 to 0.125
- pair_con: bfloat16 [16, 16, 16, 2048], P('blk', None, None, 'ga'), may hold values from -6 to 6
- screened: bfloat16 [16, 2048, 2048], P('blk', None, 'ga'), may hold values from -0.125 to 0.125
- amplitude: bfloat16 [16, 16], P('blk'), may hold values from -6 to 6
- qmap: int32 [16, 16], P('blk'), may hold values from 0 to 15, as said below
Outputs:
- kernel_x: float32 [16, 16], P('blk')
Inputs may be any that keep to these rules, and one draw needn't show every extreme that they name: qmap[k, k'] is the label of the difference k - k' (periodic) on a grid of 8 by 2 points, with the points and the differences labelled at random; every row and every column holds each label once.
All inputs are finite; a program needn't handle non-finite values.
Results may differ from a plain program's by a relative error of at most 0.004.
Values may be sent and summed in bfloat16 or wider, within the bound.
A program may use at most 64 MiB of HBM per device.

v0:
```python
import jax
import jax.numpy as jnp
from jax import lax
from jax.sharding import PartitionSpec as P

NV = 4
NC = 4


def inverse_rows(qmap):
    total = qmap.shape[1]
    labels = jnp.arange(total, dtype=jnp.int32)
    hits = (qmap[:, :, None] == labels[None, None, :]).astype(jnp.int32)
    return jnp.sum(hits * labels[None, :, None], axis=1)


def kernel_unit(sent_con, screened):
    summed = jnp.einsum(
        "kqxg,qgh->kqxh",
        lax.all_gather(sent_con, "ga", axis=3, tiled=True),
        screened,
        preferred_element_type=jnp.float32,
    )
    return summed.astype(jnp.bfloat16)


def contract(unit, zeta):
    count, labels, width = (unit.shape[0], unit.shape[1], unit.shape[3])
    unit_five = unit.reshape(count, labels, NC, NC, width)
    zeta_five = zeta.reshape(count, labels, NV, NC, width)
    terms = jnp.einsum(
        "nqcyg,nqayg->nqac", unit_five, zeta_five, preferred_element_type=jnp.float32
    )
    return terms.reshape(count, labels, NV * NC)


def body(pair_val, pair_con, screened, amplitude, qmap):
    local_k, total, band_pairs, width = pair_val.shape
    every_amp = lax.all_gather(amplitude, "blk", axis=0, tiled=True)
    partner = inverse_rows(qmap)
    val_sorted = jnp.take_along_axis(pair_val, partner[:, :, None, None], axis=1)
    con_sorted = jnp.take_along_axis(pair_con, partner[:, :, None, None], axis=1)
    amp_sorted = every_amp[partner].reshape(local_k, total, NV, NC)
    val_five = val_sorted.reshape(local_k, total, NV, NV, width)
    zeta = jnp.einsum("kqavg,kqvc->kqacg", val_five, amp_sorted, preferred_element_type=jnp.float32)
    zeta = zeta.astype(jnp.bfloat16).reshape(local_k, total, NV * NC, width)
    sent_zeta, sent_con = (
        lax.all_to_all(zeta, "blk", split_axis=1, concat_axis=0, tiled=True),
        lax.all_to_all(con_sorted, "blk", split_axis=1, concat_axis=0, tiled=True),
    )
    unit = kernel_unit(sent_con, screened)
    partial_value = contract(unit, sent_zeta)
    back = lax.all_to_all(partial_value, "blk", split_axis=0, concat_axis=1, tiled=True)
    summed = jnp.sum(back, 1)
    result = lax.psum(summed, "ga")
    return result / total


def solution(mesh):
    placed = (
        P("blk", None, None, "ga"),
        P("blk", None, None, "ga"),
        P("blk", None, "ga"),
        P("blk", None),
        P("blk", None),
    )
    return jax.shard_map(
        body, mesh=mesh, in_specs=placed, out_specs=P("blk", None), check_vma=False
    )
```

profile of v0, /device:TPU:0, one launch (start us, length us, event | category | flops | bytes accessed | tf_op | source)
XLA Modules:
  0.0 94.8 jit_solution(7691314893441121280)
XLA Ops:
  6.5 0.8 select_reduce_fusion
  7.5 0.1 copy-done
  7.6 0.6 gather_fusion.2
  8.2 1.7 %gather_fusion.1 = bf16[32,16,512]{2,1,0:T(8,128)(2,1)S(1)} fusion(bf16[2,16,16,512]{3,2,1,0:T(8,128)(2,1)} %param.7, s32[32]{0:T(128)S(1)} %reshape.94), kind=kCustom, calls=%fused_computation.clone | custom fusion | bytes 1048832 | tf_op jit(solution)/shard_map/jit(take_along_axis)/gather | solution.py:41
  9.9 0.2 broadcast_select_fusion.1
  10.1 21.6 %all_to_all.42 = bf16[2,16,16,512]{3,2,0,1:T(8,128)(2,1)S(1)} all-to-all(bf16[2,16,16,512]{3,2,0,1:T(8,128)(2,1)S(1)} %copy.53), channel_id=1, replica_groups=mesh['blk'=8,'ga'=4] {'blk'}, dimensions={1} | all-to-all | bytes 1048576 | tf_op jit(solution)/shard_map/all_to_all | solution.py:49
  31.7 0.8 copy.55
  32.7 18.6 %all-gather = bf16[8,2,16]{2,1,0:T(2,128)(2,1)S(1)} all-gather(bf16[1,2,16]{2,1,0:T(2,128)(2,1)S(1)} %bitcast.70), channel_id=1, replica_groups=mesh['blk'=8,'ga'=4] {'blk'}, dimensions={0}, use_global_device_ids=true | all-gather | bytes 576 | tf_op jit(solution)/shard_map/all_gather | solution.py:39
  51.2 0.6 gather_fusion
  51.8 0.1 copy.48
  51.9 0.1 reshape.52
  52.0 0.1 copy.62
  52.1 0.1 reshape.53
  52.3 0.4 fusion.5
  52.7 0.1 reshape.54
  52.9 13.1 %all_to_all.43 = bf16[2,16,16,512]{3,2,0,1:T(8,128)(2,1)S(1)} all-to-all(bf16[2,16,16,512]{3,2,0,1:T(8,128)(2,1)S(1)} %copy.50), channel_id=1, replica_groups=mesh['blk'=8,'ga'=4] {'blk'}, dimensions={1} | all-to-all | bytes 1048576 | tf_op jit(solution)/shard_map/all_to_all | solution.py:48
  65.9 0.5 copy.52
  66.5 4.1 %fusion.6 = bf16[16,2,16,512]{3,2,0,1:T(8,128)(2,1)S(1)} fusion(bf16[16,2,16,2048]{3,2,0,1:T(8,128)(2,1)} %all-gather.3.cloned.1.call-done, bf16[2,2048,512]{2,1,0:T(8,128)(2,1)} %param.9), kind=kOutput, calls=%fused_computation.8 | convolution fusion | flops 1074003968 | bytes 6815744 | tf_op jit(solution)/shard_map/kqxg,qgh->kqxh/dot_general | solution.py:18
  70.6 0.1 reshape.56
  70.7 0.8 convolution_bitcast_fusion
  71.5 0.1 copy.58
  71.7 10.0 %all_to_all.44 = f32[16,2,16]{2,1,0:T(2,128)S(1)} all-to-all(f32[16,2,16]{2,1,0:T(2,128)S(1)} %copy.59), channel_id=1, replica_groups=mesh['blk'=8,'ga'=4] {'blk'}, dimensions={0} | all-to-all | bytes 4096 | tf_op jit(solution)/shard_map/all_to_all | solution.py:53
  81.8 5.7 %psum.7 = f32[2,16]{1,0:T(2,128)S(1)} all-reduce(f32[2,16]{1,0:T(2,128)S(1)} %reduce_sum.31), channel_id=1, replica_groups=mesh['blk'=8,'ga'=4] {'ga'}, use_global_device_ids=true, to_apply=%region_3.0 | all-reduce | flops 32 | bytes 256 | tf_op jit(solution)/shard_map/psum | solution.py:55
  87.4 0.6 broadcast_multiply_fusion
  (16 shorter events, 0.4 us)
Async XLA Ops:
  6.5 1.1 %copy-start = (bf16[2,16,16,512]{3,2,1,0:T(8,128)(2,1)S(1)}, bf16[2,16,16,512]{3,2,1,0:T(8,128)(2,1)}, u32[]{:S(2)}) copy-start(bf16[2,16,16,512]{3,2,1,0:T(8,128)(2,1)} %param.8) | copy-start | bytes 1572868
  6.5 26.1 %copy-start.1 = (bf16[2,16]{1,0:T(2,128)(2,1)S(1)}, bf16[2,16]{1,0:T(2,128)(2,1)}, u32[]{:S(2)}) copy-start(bf16[2,16]{1,0:T(2,128)(2,1)} %param.10) | copy-start | bytes 196
  6.5 60.0 %all-gather.3.cloned.1.call-start = ((), (), s32[]{:S(2)}) async-start(), calls=%async_computation.3 | async-start | bytes 2621440 | tf_op jit(solution)/shard_map/all_gather | solution.py:20
Sparse Core Ops, SparseCore 0:
  32.7 21.5 all-gather.2
where the time goes:
time: 95.2 us; the launch traced here: 94.8 us
  blocking collectives  68.9 us (72%)
  between operations  13.5 us (14%)
  local copies, waits for them, and re-layouts  5.52 us (6%)
  matrix products  5.27 us (6%)
  other arithmetic  1.62 us (2%)
    all_to_all x1, blocking collectives, body(): lax.all_to_all(con_sorted, 'blk', split_axis=1, concat_axis=0, tiled=True)  21.6 us
    all_gather x1, blocking collectives, body(): every_amp = lax.all_gather(amplitude, 'blk', axis=0, tiled=True)  18.6 us
    all_to_all x1, blocking collectives, body(): lax.all_to_all(zeta, 'blk', split_axis=1, concat_axis=0, tiled=True)  13.1 us
    all_to_all x1, blocking collectives, body(): lax.all_to_all(partial_value, 'blk', split_axis=0, concat_axis=1, tiled=T...  10 us
    psum x1, blocking collectives, body(): result = lax.psum(summed, 'ga')  5.66 us
    dot_general x1, matrix products, kernel_unit(): jnp.einsum('kqxg,qgh->kqxh', lax.all_gather(sent_con, 'ga', axis=3, tiled...  4.07 us
  transfers between devices with their start and end apart: 1, of which 0 were waited for; matrix products, arithmetic and copies ran while one was open for 2% of the time, Pallas kernels for 0%

commit v1 on v0

v1 whole, which is shorter than its diff:
```python
import functools

import jax
import jax.numpy as jnp
from jax import lax
from jax.experimental import pallas as pl
from jax.experimental.pallas import tpu as pltpu
from jax.sharding import PartitionSpec as P

NV = 4
NC = 4
ROWS = 16
TILE = 256
MESH = pl.DeviceIdType.MESH
F32 = jnp.float32
BF16 = jnp.bfloat16


def iota(shape, dim):
    return lax.broadcasted_iota(jnp.int32, shape, dim)


def one_hot(mask):
    return jnp.where(mask, 1.0, 0.0).astype(F32)


def kernel(
    blks, gas, val_hbm, con_hbm, w_hbm, amp_ref, q_ref, out_ref,
    val_in, con_in, w_in, con_send, zeta_send, con_all, zeta_all, amp_all, amp_rows, unit, contrib, fin,
    load_sem, amp_ssem, amp_rsem, con_ssem, con_rsem, zeta_ssem, zeta_rsem,
    row_ssem, row_rsem, core_ssem, core_rsem, fin_ssem, fin_rsem,
):
    me, ga = lax.axis_index("blk"), lax.axis_index("ga")
    local_k, total = q_ref.shape
    labels, width = w_in.shape[0], w_in.shape[2]
    wide = total * ROWS
    lane = me * gas + ga
    devices = blks * gas
    rings = gas // 2
    other = ga + 1 - 2 * (ga % 2)

    loads = [
        pltpu.make_async_copy(con_hbm, con_in, load_sem.at[0]),
        pltpu.make_async_copy(val_hbm, val_in, load_sem.at[1]),
        pltpu.make_async_copy(w_hbm, w_in, load_sem.at[2]),
    ]
    for load in loads:
        load.start()

    barrier = pltpu.get_barrier_semaphore()

    def greet(i, carry):
        to = (lane + i) % devices
        pl.semaphore_signal(barrier, inc=1, device_id=(to // gas, to % gas), device_id_type=MESH)
        return carry

    lax.fori_loop(1, devices, greet, 0)

    def amp_copy(step):
        return pltpu.make_async_remote_copy(
            src_ref=amp_ref, dst_ref=amp_all.at[me],
            send_sem=amp_ssem.at[step], recv_sem=amp_rsem.at[step],
            device_id=((me + step) % blks, ga), device_id_type=MESH)

    def con_copy(step):
        to = (me + step) % blks
        return pltpu.make_async_remote_copy(
            src_ref=con_send.at[to], dst_ref=con_all.at[ga, me],
            send_sem=con_ssem.at[step], recv_sem=con_rsem.at[step],
            device_id=(to, ga), device_id_type=MESH)

    def zeta_copy(step):
        to = (me + step) % blks
        return pltpu.make_async_remote_copy(
            src_ref=zeta_send.at[to], dst_ref=zeta_all.at[me],
            send_sem=zeta_ssem.at[step], recv_sem=zeta_rsem.at[step],
            device_id=(to, ga), device_id_type=MESH)

    def row_copy(hop, step):
        owner = (me + blks - step) % blks
        return pltpu.make_async_remote_copy(
            src_ref=con_all.at[ga, owner], dst_ref=con_all.at[ga, owner],
            send_sem=row_ssem.at[hop, step], recv_sem=row_rsem.at[hop, step],
            device_id=(me, (ga + 2 * hop) % gas), device_id_type=MESH)

    def core_copy(hop, step):
        owner = (me + blks - step) % blks
        part = (ga + gas - 2 * hop) % gas
        return pltpu.make_async_remote_copy(
            src_ref=con_all.at[part, owner], dst_ref=con_all.at[part, owner],
            send_sem=core_ssem.at[hop, step], recv_sem=core_rsem.at[hop, step],
            device_id=(me, other), device_id_type=MESH)

    def order(i):
        return (blks // 2 + i - 1) % (blks - 1) + 1

    def each_step(action):
        def run(i, carry):
            action(order(i))
            return carry

        lax.fori_loop(0, blks - 1, run, 0)

    spread = one_hot(iota((total, wide), 1) >> 4 == iota((total, wide), 0)).astype(BF16)
    labels_at = jnp.dot(q_ref[...].astype(F32).astype(BF16), spread, preferred_element_type=F32).astype(jnp.int32)
    row, col = iota((TILE, wide), 0), iota((TILE, wide), 1)
    same_pair = (row & 15) == (col & 15)
    same_band = ((row >> 2) & 3) == ((col >> 2) & 3)
    chunk_labels = TILE // ROWS
    chunk_blks = chunk_labels // labels

    def stored(ref, k, chunk, value):
        blocks = value.astype(BF16).reshape(chunk_blks, labels, ROWS, width)
        ref[pl.ds(chunk * chunk_blks, chunk_blks), :, pl.ds(k * ROWS, ROWS), :] = blocks

    hits = {}
    for k in range(local_k):
        for chunk in range(wide // TILE):
            hits[k, chunk] = labels_at[k : k + 1, :] == (row >> 4) + chunk * chunk_labels
    loads[0].wait()
    for k in range(local_k):
        con_k = con_in[k].reshape(wide, width)
        for chunk in range(wide // TILE):
            pick = one_hot(hits[k, chunk] & same_pair).astype(BF16)
            stored(con_send, k, chunk, jnp.dot(pick, con_k, preferred_element_type=F32))
    con_all[ga, me] = con_send[me]
    amp_all[me] = amp_ref[...]

    pl.semaphore_wait(barrier, devices - 1)
    each_step(lambda step: amp_copy(step).start())
    each_step(lambda step: con_copy(step).start())
    for hop in range(1, rings):
        row_copy(hop, 0).start()
    core_copy(0, 0).start()

    each_step(lambda step: amp_copy(step).wait_recv())
    for blk in range(blks):
        amp_rows[pl.ds(blk * local_k, local_k), :] = amp_all[blk].astype(F32)
    amps = lax.dot_general(
        amp_rows[...].astype(BF16), spread, (((0,), (0,)), ((), ())), preferred_element_type=F32)
    pair, at = iota((NV * NC, wide), 0), iota((NV * NC, wide), 1)
    amps = jnp.where((pair >> 2) == (at & 3), amps, 0.0).astype(BF16)
    lines, pairs = iota((TILE, NV * NC), 0), iota((TILE, NV * NC), 1)
    amps = jnp.dot(one_hot((lines & 3) == (pairs & 3)).astype(BF16), amps, preferred_element_type=F32)
    amps = jnp.where(same_band, amps, 0.0)
    loads[1].wait()
    for k in range(local_k):
        val_k = val_in[k].reshape(wide, width)
        for chunk in range(wide // TILE):
            mix = jnp.where(hits[k, chunk], amps, 0.0).astype(BF16)
            stored(zeta_send, k, chunk, jnp.dot(mix, val_k, preferred_element_type=F32))
    zeta_all[me] = zeta_send[me]
    each_step(lambda step: zeta_copy(step).start())

    def relay(i, carry):
        step = order(i)
        con_copy(step).wait_recv()
        for hop in range(1, rings):
            row_copy(hop, step).start()
        core_copy(0, step).start()
        before = jnp.where(i == 0, 0, order(jnp.maximum(i - 1, 0)))
        for hop in range(1, rings):
            row_copy(hop, before).wait_recv()
            core_copy(hop, before).start()
        return carry

    lax.fori_loop(0, blks - 1, relay, 0)
    last = (blks // 2 + blks - 3) % (blks - 1) + 1
    for hop in range(1, rings):
        row_copy(hop, last).wait_recv()
        core_copy(hop, last).start()

    def gathered(step, carry):
        for hop in range(rings):
            core_copy(hop, step).wait_recv()
        return carry

    loads[2].wait()
    lax.fori_loop(0, blks, gathered, 0)

    group = TILE // (local_k * ROWS)
    for part in range(blks // group):
        for label in range(labels):
            summed = None
            for quarter in range(gas):
                cons = con_all[quarter, pl.ds(part * group, group), label].reshape(TILE, width)
                term = jnp.dot(cons, w_in[label, pl.ds(quarter * width, width), :], preferred_element_type=F32)
                summed = term if summed is None else summed + term
            unit[label, pl.ds(part * TILE, TILE), :] = summed.astype(BF16)

    each_step(lambda step: zeta_copy(step).wait_recv())

    r, s = iota((TILE, TILE), 0), iota((TILE, TILE), 1)
    kept = ((r >> 4) == (s >> 4)) & ((r & 3) == (s & 3))
    c_at, w_of = iota((ROWS, 128), 0), iota((ROWS, 128), 1)
    by_c = one_hot(((c_at >> 2) == (w_of & 3)) & (w_of < ROWS))
    s_at, w_at = iota((TILE, 128), 0), iota((TILE, 128), 1)
    by_v = ((s_at >> 2) & 3) == (w_at >> 2)
    slot, of = iota((group * 8, TILE), 0), iota((group * 8, TILE), 1)
    by_k = one_hot(((slot & 7) < local_k) & ((of >> 4) == (slot >> 3) * local_k + (slot & 7)))
    for part in range(blks // group):
        cross = None
        for label in range(labels):
            zetas = zeta_all[pl.ds(part * group, group), label].reshape(TILE, width)
            term = lax.dot_general(
                unit[label, pl.ds(part * TILE, TILE), :], zetas, (((1,), (1,)), ((), ())),
                preferred_element_type=F32)
            cross = term if cross is None else cross + term
        folded = jnp.sum(jnp.where(kept, cross, 0.0).reshape(TILE // ROWS, ROWS, TILE), axis=0)
        spread_c = lax.dot_general(
            folded, by_c, (((0,), (0,)), ((), ())), precision=lax.Precision.HIGHEST, preferred_element_type=F32)
        spread_c = jnp.where(by_v, spread_c, 0.0)
        per_k = jnp.dot(by_k, spread_c, precision=lax.Precision.HIGHEST, preferred_element_type=F32)
        contrib[pl.ds(part * group, group)] = per_k.reshape(group, 8, 128)

    def fin_copy(i):
        to = (lane + i) % devices
        return pltpu.make_async_remote_copy(
            src_ref=contrib.at[to // gas], dst_ref=fin.at[i],
            send_sem=fin_ssem.at[i], recv_sem=fin_rsem.at[i],
            device_id=(to // gas, to % gas), device_id_type=MESH)

    def every(action):
        def run(i, carry):
            action(fin_copy(i))
            return carry

        lax.fori_loop(1, devices, run, 0)

    every(lambda copy: copy.start())
    fin[0] = contrib[me]

    each_step(lambda step: amp_copy(step).wait_send())
    each_step(lambda step: con_copy(step).wait_send())
    each_step(lambda step: zeta_copy(step).wait_send())

    def relayed(step, carry):
        for hop in range(1, rings):
            row_copy(hop, step).wait_send()
        for hop in range(rings):
            core_copy(hop, step).wait_send()
        return carry

    lax.fori_loop(0, blks, relayed, 0)
    every(lambda copy: copy.wait())
    out_ref[...] = jnp.sum(fin[...], axis=0)[:local_k, :ROWS] / total


def body(pair_val, pair_con, screened, amplitude, qmap, *, blks, gas):
    local_k, total, _, width = pair_val.shape
    labels, depth, _ = screened.shape
    devices = blks * gas
    dma = pltpu.SemaphoreType.DMA
    anywhere = pl.BlockSpec(memory_space=pl.ANY)
    vmem = pl.BlockSpec(memory_space=pltpu.VMEM)
    block = (labels, local_k * ROWS, width)
    return pl.pallas_call(
        functools.partial(kernel, blks, gas),
        out_shape=jax.ShapeDtypeStruct((local_k, NV * NC), F32),
        in_specs=[anywhere, anywhere, anywhere, vmem, vmem],
        out_specs=vmem,
        scratch_shapes=[
            pltpu.VMEM(pair_val.shape, BF16),
            pltpu.VMEM(pair_con.shape, BF16),
            pltpu.VMEM(screened.shape, BF16),
            pltpu.VMEM((blks,) + block, BF16),
            pltpu.VMEM((blks,) + block, BF16),
            pltpu.VMEM((gas, blks) + block, BF16),
            pltpu.VMEM((blks,) + block, BF16),
            pltpu.VMEM((blks,) + amplitude.shape, BF16),
            pltpu.VMEM((total, NV * NC), F32),
            pltpu.VMEM((labels, total * ROWS, width), BF16),
            pltpu.VMEM((blks, 8, 128), F32),
            pltpu.VMEM((devices, 8, 128), F32),
            dma((3,)),
            dma((blks,)), dma((blks,)), dma((blks,)), dma((blks,)), dma((blks,)), dma((blks,)),
            dma((gas // 2, blks)), dma((gas // 2, blks)), dma((gas // 2, blks)), dma((gas // 2, blks)),
            dma((devices,)), dma((devices,)),
        ],
        compiler_params=pltpu.CompilerParams(
            collective_id=0, has_side_effects=True, vmem_limit_bytes=60 * 1024 * 1024),
    )(pair_val, pair_con, screened, amplitude, qmap)


def solution(mesh):
    placed = (
        P("blk", None, None, "ga"),
        P("blk", None, None, "ga"),
        P("blk", None, "ga"),
        P("blk", None),
        P("blk", None),
    )
    sizes = {"blks": mesh.shape["blk"], "gas": mesh.shape["ga"]}
    return jax.shard_map(
        functools.partial(body, **sizes), mesh=mesh, in_specs=placed, out_specs=P("blk", None), check_vma=False
    )
```

time: 95.2 us -> 43 us (0.45)
  blocking collectives: 68.9 us -> 0 us
  Pallas kernels: 0 us -> 41.6 us
  between operations: 13.5 us -> 0.01 us
  matrix products: 5.27 us -> 0 us
  local copies, waits for them, and re-layouts: 5.52 us -> 1.24 us
  other arithmetic: 1.62 us -> 0 us
    all_to_all x3 -> x0, blocking collectives: 44.7 us -> none  [the longest x1 21.6 us: body(): lax.all_to_all(con_sorted, 'blk', split_axis=1, concat_axis=0, tiled=True)]
    pallas_call x0 -> x1, Pallas kernels: none -> 41.6 us  [body(): pl.pallas_call(functools.partial(kernel, blks, gas), out_shape=jax.ShapeD...]
    all_gather x1 -> x0, blocking collectives: 18.6 us -> none  [body(): every_amp = lax.all_gather(amplitude, 'blk', axis=0, tiled=True)]
    psum x1 -> x0, blocking collectives: 5.66 us -> none  [body(): result = lax.psum(summed, 'ga')]
    dot_general x3 -> x0, matrix products: 5.27 us -> none  [the longest x1 4.07 us: kernel_unit(): jnp.einsum('kqxg,qgh->kqxh', lax.all_gather(sent_con, 'ga', axis=3, tiled...]
    gather x5 -> x0, local copies, waits for them, and re-layouts: 3.04 us -> none  [the longest x2 1.75 us: body(): jnp.take_along_axis(pair_val, partner[:, :, None, None], axis=1)]
    all_to_all x2 -> x0, local copies, waits for them, and re-layouts: 1.38 us -> none  [the longest x1 0.83 us: body(): lax.all_to_all(con_sorted, 'blk', split_axis=1, concat_axis=0, tiled=True)]
    unnamed x4 -> x1, local copies, waits for them, and re-layouts: 0.13 us -> 1.24 us
  transfers between devices with their start and end apart: 1 -> 0, of which waited for: 0 -> 0; matrix products, arithmetic and copies ran while one was open for 2% -> 0% of each run, Pallas kernels for 0% -> 0%
where the time goes in v1:
time: 43 us; the launch traced here: 42.8 us
  Pallas kernels  41.6 us (97%)
  local copies, waits for them, and re-layouts  1.24 us (3%)
    pallas_call x1, Pallas kernels, body(): pl.pallas_call(functools.partial(kernel, blks, gas), out_shape=jax.ShapeD...  41.6 us
    unnamed x1, local copies, waits for them, and re-layouts  1.24 us

profile of v1, /device:TPU:0, one launch (start us, length us, event | category | flops | bytes accessed | tf_op | source)
XLA Modules:
  0.0 42.8 jit_solution(11710257650886688760)
XLA Ops:
  0.0 41.6 %shard_map.55 = f32[2,16]{1,0:T(2,128)} custom-call(bf16[2,16,16,512]{3,2,1,0:T(8,128)(2,1)} %val_hbm.1, bf16[2,16,16,512]{3,2,1,0:T(8,128)(2,1)} %con_hbm.1, bf16[2,2048,512]{2,1,0:T(8,128)(2,1)} %w_hbm.1, bf16[2,16]{1,0:T(2,128)(2,1)} %amp_ref.1, s32[2,16]{1,0:T(2,128)} %q_ref.1), custom_call_target="tpu_custom_call" | custom-call | tf_op jit(solution)/shard_map/pallas_call | solution.py:257
  41.6 1.2 %copy.7 = f32[2,16]{1,0:T(2,128)} copy(f32[2,16]{1,0:T(2,128)} %shard_map.55) | data formatting | bytes 256

commit v2 on v1

--- a/solution.py
+++ b/solution.py
@@ -28,7 +28,7 @@
     blks, gas, val_hbm, con_hbm, w_hbm, amp_ref, q_ref, out_ref,
     val_in, con_in, w_in, con_send, zeta_send, con_all, zeta_all, amp_all, amp_rows, unit, contrib, fin,
     load_sem, amp_ssem, amp_rsem, con_ssem, con_rsem, zeta_ssem, zeta_rsem,
-    row_ssem, row_rsem, core_ssem, core_rsem, fin_ssem, fin_rsem,
+    row_ssem, row_rsem, core_ssem, core_rsem, fin_ssem, fin_rsem, hop_sem,
 ):
     me, ga = lax.axis_index("blk"), lax.axis_index("ga")
     local_k, total = q_ref.shape
@@ -47,59 +47,110 @@
     for load in loads:
         load.start()
 
+    line = blks // 2
+    z, x = me // 2, me % 2
+    shifts = [(0, 1)]
+    for far in range(1, line):
+        shifts += [(far, 0), (-far, 0), (far, 1), (-far, 1)]
+    shifts.sort(key=lambda shift: abs(shift[0]) + shift[1])
+
+    def reach(shift):
+        return abs(shift[0]) + shift[1]
+
+    def index_of(shift):
+        return (shift[0] + line - 1) * 2 + shift[1]
+
+    def to_blk(shift):
+        return (z + shift[0]) * 2 + (x + shift[1]) % 2
+
+    def from_blk(shift):
+        return (z - shift[0]) * 2 + (x + shift[1]) % 2
+
+    def sent(chosen, action):
+        for shift in chosen:
+            pl.when((z + shift[0] >= 0) & (z + shift[0] < line))(functools.partial(action, shift))
+
+    def received(chosen, action):
+        for shift in chosen:
+            pl.when((z - shift[0] >= 0) & (z - shift[0] < line))(functools.partial(action, shift))
+
+    beside = jnp.minimum(z, 1) + jnp.minimum(line - 1 - z, 1)
     barrier = pltpu.get_barrier_semaphore()
 
-    def greet(i, carry):
-        to = (lane + i) % devices
-        pl.semaphore_signal(barrier, inc=1, device_id=(to // gas, to % gas), device_id_type=MESH)
-        return carry
-
-    lax.fori_loop(1, devices, greet, 0)
-
-    def amp_copy(step):
+    def greet(semaphore):
+        for far in (1, -1):
+            @pl.when((z + far >= 0) & (z + far < line))
+            def _():
+                pl.semaphore_signal(semaphore, inc=1, device_id=(me + 2 * far, ga), device_id_type=MESH)
+
+    greet(barrier)
+    pl.semaphore_signal(barrier, inc=1, device_id=(z * 2 + (x + 1) % 2, ga), device_id_type=MESH)
+    pl.semaphore_signal(barrier, inc=1, device_id=(me, other), device_id_type=MESH)
+    for hop in range(1, rings):
+        pl.semaphore_signal(barrier, inc=1, device_id=(me, (ga + 2 * hop) % gas), device_id_type=MESH)
+
+    def amp_copy(shift):
+        at = index_of(shift)
         return pltpu.make_async_remote_copy(
             src_ref=amp_ref, dst_ref=amp_all.at[me],
-            send_sem=amp_ssem.at[step], recv_sem=amp_rsem.at[step],
-            device_id=((me + step) % blks, ga), device_id_type=MESH)
-
-    def con_copy(step):
-        to = (me + step) % blks
-        return pltpu.make_async_remote_copy(
-            src_ref=con_send.at[to], dst_ref=con_all.at[ga, me],
-            send_sem=con_ssem.at[step], recv_sem=con_rsem.at[step],
-            device_id=(to, ga), device_id_type=MESH)
-
-    def zeta_copy(step):
-        to = (me + step) % blks
-        return pltpu.make_async_remote_copy(
-            src_ref=zeta_send.at[to], dst_ref=zeta_all.at[me],
-            send_sem=zeta_ssem.at[step], recv_sem=zeta_rsem.at[step],
-            device_id=(to, ga), device_id_type=MESH)
-
-    def row_copy(hop, step):
-        owner = (me + blks - step) % blks
+            send_sem=amp_ssem.at[at], recv_sem=amp_rsem.at[at],
+            device_id=(to_blk(shift), ga), device_id_type=MESH)
+
+    def con_copy(shift):
+        at = index_of(shift)
+        return pltpu.make_async_remote_copy(
+            src_ref=con_send.at[to_blk(shift)], dst_ref=con_all.at[ga, me],
+            send_sem=con_ssem.at[at], recv_sem=con_rsem.at[at],
+            device_id=(to_blk(shift), ga), device_id_type=MESH)
+
+    def zeta_copy(shift):
+        at = index_of(shift)
+        return pltpu.make_async_remote_copy(
+            src_ref=zeta_send.at[to_blk(shift)], dst_ref=zeta_all.at[me],
+            send_sem=zeta_ssem.at[at], recv_sem=zeta_rsem.at[at],
+            device_id=(to_blk(shift), ga), device_id_type=MESH)
+
+    def arrival(ref, semaphores, shift):
+        at = index_of(shift)
+        return pltpu.make_async_remote_copy(
+            src_ref=ref, dst_ref=ref, send_sem=con_ssem.at[at], recv_sem=semaphores.at[at],
+            device_id=(from_blk(shift), ga), device_id_type=MESH)
+
+    def amp_arrival(shift):
+        return arrival(amp_all.at[from_blk(shift)], amp_rsem, shift)
+
+    def con_arrival(shift):
+        return arrival(con_all.at[ga, from_blk(shift)], con_rsem, shift)
+
+    def zeta_arrival(shift):
+        return arrival(zeta_all.at[from_blk(shift)], zeta_rsem, shift)
+
+    def row_copy(hop, owner, at):
         return pltpu.make_async_remote_copy(
             src_ref=con_all.at[ga, owner], dst_ref=con_all.at[ga, owner],
-            send_sem=row_ssem.at[hop, step], recv_sem=row_rsem.at[hop, step],
+            send_sem=row_ssem.at[hop, at], recv_sem=row_rsem.at[hop, at],
             device_id=(me, (ga + 2 * hop) % gas), device_id_type=MESH)
 
-    def core_copy(hop, step):
-        owner = (me + blks - step) % blks
+    def core_copy(hop, owner, at):
         part = (ga + gas - 2 * hop) % gas
         return pltpu.make_async_remote_copy(
             src_ref=con_all.at[part, owner], dst_ref=con_all.at[part, owner],
-            send_sem=core_ssem.at[hop, step], recv_sem=core_rsem.at[hop, step],
+            send_sem=core_ssem.at[hop, at], recv_sem=core_rsem.at[hop, at],
             device_id=(me, other), device_id_type=MESH)
 
-    def order(i):
-        return (blks // 2 + i - 1) % (blks - 1) + 1
-
-    def each_step(action):
-        def run(i, carry):
-            action(order(i))
-            return carry
-
-        lax.fori_loop(0, blks - 1, run, 0)
+    def hand_on(owner, at):
+        for hop in range(1, rings):
+            row_copy(hop, owner, at).start()
+        core_copy(0, owner, at).start()
+
+    def across(owner, at):
+        for hop in range(1, rings):
+            row_copy(hop, owner, at).wait_recv()
+            core_copy(hop, owner, at).start()
+
+    def relay(shift):
+        con_arrival(shift).wait_recv()
+        hand_on(from_blk(shift), index_of(shift))
 
     spread = one_hot(iota((total, wide), 1) >> 4 == iota((total, wide), 0)).astype(BF16)
     labels_at = jnp.dot(q_ref[...].astype(F32).astype(BF16), spread, preferred_element_type=F32).astype(jnp.int32)
@@ -126,14 +177,21 @@
     con_all[ga, me] = con_send[me]
     amp_all[me] = amp_ref[...]
 
-    pl.semaphore_wait(barrier, devices - 1)
-    each_step(lambda step: amp_copy(step).start())
-    each_step(lambda step: con_copy(step).start())
-    for hop in range(1, rings):
-        row_copy(hop, 0).start()
-    core_copy(0, 0).start()
-
-    each_step(lambda step: amp_copy(step).wait_recv())
+    pl.semaphore_wait(barrier, beside + rings + 1)
+    for phase in range(1, line + 1):
+        if phase > 1:
+            greet(hop_sem.at[phase])
+            pl.semaphore_wait(hop_sem.at[phase], beside)
+        near = [shift for shift in shifts if reach(shift) == phase]
+        sent(near, lambda shift: amp_copy(shift).start())
+        sent(near, lambda shift: con_copy(shift).start())
+        if phase == 1:
+            hand_on(me, 2 * line - 2)
+    near = [shift for shift in shifts if reach(shift) == 1]
+    rest = [shift for shift in shifts if reach(shift) > 1]
+    received(near, relay)
+
+    received(shifts, lambda shift: amp_arrival(shift).wait_recv())
     for blk in range(blks):
         amp_rows[pl.ds(blk * local_k, local_k), :] = amp_all[blk].astype(F32)
     amps = lax.dot_general(
@@ -150,33 +208,19 @@
             mix = jnp.where(hits[k, chunk], amps, 0.0).astype(BF16)
             stored(zeta_send, k, chunk, jnp.dot(mix, val_k, preferred_element_type=F32))
     zeta_all[me] = zeta_send[me]
-    each_step(lambda step: zeta_copy(step).start())
-
-    def relay(i, carry):
-        step = order(i)
-        con_copy(step).wait_recv()
-        for hop in range(1, rings):
-            row_copy(hop, step).start()
-        core_copy(0, step).start()
-        before = jnp.where(i == 0, 0, order(jnp.maximum(i - 1, 0)))
-        for hop in range(1, rings):
-            row_copy(hop, before).wait_recv()
-            core_copy(hop, before).start()
-        return carry
-
-    lax.fori_loop(0, blks - 1, relay, 0)
-    last = (blks // 2 + blks - 3) % (blks - 1) + 1
-    for hop in range(1, rings):
-        row_copy(hop, last).wait_recv()
-        core_copy(hop, last).start()
-
-    def gathered(step, carry):
+    sent(shifts[::-1], lambda shift: zeta_copy(shift).start())
+
+    received(rest, relay)
+    across(me, 2 * line - 2)
+    received(shifts, lambda shift: across(from_blk(shift), index_of(shift)))
+
+    def gathered(owner, at):
         for hop in range(rings):
-            core_copy(hop, step).wait_recv()
-        return carry
+            core_copy(hop, owner, at).wait_recv()
 
     loads[2].wait()
-    lax.fori_loop(0, blks, gathered, 0)
+    gathered(me, 2 * line - 2)
+    received(shifts, lambda shift: gathered(from_blk(shift), index_of(shift)))
 
     group = TILE // (local_k * ROWS)
     for part in range(blks // group):
@@ -188,16 +232,14 @@
                 summed = term if summed is None else summed + term
             unit[label, pl.ds(part * TILE, TILE), :] = summed.astype(BF16)
 
-    each_step(lambda step: zeta_copy(step).wait_recv())
+    received(shifts, lambda shift: zeta_arrival(shift).wait_recv())
 
     r, s = iota((TILE, TILE), 0), iota((TILE, TILE), 1)
     kept = ((r >> 4) == (s >> 4)) & ((r & 3) == (s & 3))
     c_at, w_of = iota((ROWS, 128), 0), iota((ROWS, 128), 1)
-    by_c = one_hot(((c_at >> 2) == (w_of & 3)) & (w_of < ROWS))
+    by_c = one_hot((c_at >> 2) == (w_of & 3))
     s_at, w_at = iota((TILE, 128), 0), iota((TILE, 128), 1)
-    by_v = ((s_at >> 2) & 3) == (w_at >> 2)
-    slot, of = iota((group * 8, TILE), 0), iota((group * 8, TILE), 1)
-    by_k = one_hot(((slot & 7) < local_k) & ((of >> 4) == (slot >> 3) * local_k + (slot & 7)))
+    by_v = (((s_at >> 2) & 3) == ((w_at >> 2) & 3)) & ((s_at >> 4) % local_k == (w_at >> 4))
     for part in range(blks // group):
         cross = None
         for label in range(labels):
@@ -210,8 +252,9 @@
         spread_c = lax.dot_general(
             folded, by_c, (((0,), (0,)), ((), ())), precision=lax.Precision.HIGHEST, preferred_element_type=F32)
         spread_c = jnp.where(by_v, spread_c, 0.0)
-        per_k = jnp.dot(by_k, spread_c, precision=lax.Precision.HIGHEST, preferred_element_type=F32)
-        contrib[pl.ds(part * group, group)] = per_k.reshape(group, 8, 128)
+        per_k = jnp.sum(spread_c.reshape(group, TILE // group, 128), axis=1)
+        for at in range(group):
+            contrib[part * group + at] = per_k[at : at + 1]
 
     def fin_copy(i):
         to = (lane + i) % devices
@@ -230,20 +273,22 @@
     every(lambda copy: copy.start())
     fin[0] = contrib[me]
 
-    each_step(lambda step: amp_copy(step).wait_send())
-    each_step(lambda step: con_copy(step).wait_send())
-    each_step(lambda step: zeta_copy(step).wait_send())
-
-    def relayed(step, carry):
+    sent(shifts, lambda shift: amp_copy(shift).wait_send())
+    sent(shifts, lambda shift: con_copy(shift).wait_send())
+    sent(shifts, lambda shift: zeta_copy(shift).wait_send())
+
+    def relayed(owner, at):
         for hop in range(1, rings):
-            row_copy(hop, step).wait_send()
+            row_copy(hop, owner, at).wait_send()
         for hop in range(rings):
-            core_copy(hop, step).wait_send()
-        return carry
-
-    lax.fori_loop(0, blks, relayed, 0)
+            core_copy(hop, owner, at).wait_send()
+
+    relayed(me, 2 * line - 2)
+    received(shifts, lambda shift: relayed(from_blk(shift), index_of(shift)))
     every(lambda copy: copy.wait())
-    out_ref[...] = jnp.sum(fin[...], axis=0)[:local_k, :ROWS] / total
+    total_row = jnp.sum(fin[...], axis=0) / total
+    for k in range(local_k):
+        out_ref[k : k + 1, :] = total_row[:, k * ROWS : (k + 1) * ROWS]
 
 
 def body(pair_val, pair_con, screened, amplitude, qmap, *, blks, gas):
@@ -270,12 +315,13 @@
             pltpu.VMEM((blks,) + amplitude.shape, BF16),
             pltpu.VMEM((total, NV * NC), F32),
             pltpu.VMEM((labels, total * ROWS, width), BF16),
-            pltpu.VMEM((blks, 8, 128), F32),
-            pltpu.VMEM((devices, 8, 128), F32),
+            pltpu.VMEM((blks, 1, 128), F32),
+            pltpu.VMEM((devices, 1, 128), F32),
             dma((3,)),
-            dma((blks,)), dma((blks,)), dma((blks,)), dma((blks,)), dma((blks,)), dma((blks,)),
-            dma((gas // 2, blks)), dma((gas // 2, blks)), dma((gas // 2, blks)), dma((gas // 2, blks)),
+            *[dma((2 * blks - 2,))] * 6,
+            *[dma((gas // 2, 2 * blks - 2))] * 4,
             dma((devices,)), dma((devices,)),
+            pltpu.SemaphoreType.REGULAR((blks // 2 + 1,)),
         ],
         compiler_params=pltpu.CompilerParams(
             collective_id=0, has_side_effects=True, vmem_limit_bytes=60 * 1024 * 1024),

time: 43 us -> 39.7 us (0.923)
  Pallas kernels: 41.6 us -> 38.3 us
    pallas_call x1, Pallas kernels: 41.6 us -> 38.3 us  [body(): pl.pallas_call(functools.partial(kernel, blks, gas), out_shape=jax.ShapeD...]
where the time goes in v2:
time: 39.7 us; the launch traced here: 39.5 us
  Pallas kernels  38.3 us (96%)
  local copies, waits for them, and re-layouts  1.24 us (3%)
    pallas_call x1, Pallas kernels, body(): pl.pallas_call(functools.partial(kernel, blks, gas), out_shape=jax.ShapeD...  38.3 us
    unnamed x1, local copies, waits for them, and re-layouts  1.24 us

profile of v2, /device:TPU:0, one launch (start us, length us, event | category | flops | bytes accessed | tf_op | source)
XLA Modules:
  0.0 39.5 jit_solution(2166468932992231309)
XLA Ops:
  0.0 38.3 %shard_map.55 = f32[2,16]{1,0:T(2,128)} custom-call(bf16[2,16,16,512]{3,2,1,0:T(8,128)(2,1)} %val_hbm.1, bf16[2,16,16,512]{3,2,1,0:T(8,128)(2,1)} %con_hbm.1, bf16[2,2048,512]{2,1,0:T(8,128)(2,1)} %w_hbm.1, bf16[2,16]{1,0:T(2,128)(2,1)} %amp_ref.1, s32[2,16]{1,0:T(2,128)} %q_ref.1), custom_call_target="tpu_custom_call" | custom-call | tf_op jit(solution)/shard_map/pallas_call | solution.py:302
  38.3 1.2 %copy.7 = f32[2,16]{1,0:T(2,128)} copy(f32[2,16]{1,0:T(2,128)} %shard_map.55) | data formatting | bytes 256
